TPU v7x, 512 devices: a whole 4x8x8 slice. The times are simulated.
512 devices in a mesh: gx: 64 (over y, z), gy: 8 (over x, core).
Axes of the slice: x: 4, y: 8, z: 8, core: 2. Of those that a mesh axis runs over, the one named last changes fastest.
Arguments:
- droplets: float32 [2, 32, 128, 4096], P(None, None, 'gx', 'gy'), as said below
- moves: int32 [2, 32, 128, 4096], P(None, None, 'gx', 'gy'), may hold values from 0 to 8, as said below
- pairing: int32 [2, 32, 128, 4096], P(None, None, 'gx', 'gy'), may hold values from 0 to 31, as said below
- collisions: int32 [2, 16, 128, 4096], P(None, None, 'gx', 'gy'), may hold values from 0 to 3
Outputs:
- droplets_out: float32 [2, 32, 128, 4096], P(None, None, 'gx', 'gy')
- moments: float32 [2, 2, 16], replicated
Inputs may be any that keep to these rules, and one draw needn't show every extreme that they name: `droplets`: entry 0 holds whole-number multiplicities from 24 to below 300, entry 1 masses from 0.05 to 2. `moves`: A code c means a step of c // 3 - 1 along x and c % 3 - 1 along y. In each step, slot and level, all droplets of one y-row take the same x-step and all droplets landing in one x-column take the same y-step, so every cell and slot receives exactly one droplet. `pairing`: for each step and cell, the entries along the slot dimension are a permutation of 0 to 31.
All inputs are finite; a program needn't handle non-finite values.
Results may differ from a plain program's by a relative error of at most 0.0003.
Values sent between devices are 32-bit elements; how exact they have to be, the bound alone decides.
A program may use at most 64 MiB of HBM per device.

v0:
```python
import jax
import jax.numpy as jnp
from jax import lax
from jax.sharding import Mesh
from jax.sharding import PartitionSpec as P

LEVELS = 16
GY = ("gy_0", "gy_1")
GX = ("gx_0", "gx_1")
GX_GY = ("gx_0", "gx_1", "gy_0", "gy_1")
count_unit = 4096.0


def padded(array, sides, width):
    for axis, dim in sides:
        size, length = (lax.axis_size(axis), array.shape[dim])
        up = [(i, (i + 1) % size) for i in range(size)]
        down = [(j, i) for i, j in up]
        last = lax.slice_in_dim(array, length - width, length, axis=dim)
        leading = lax.slice_in_dim(array, 0, width, axis=dim)
        before = lax.ppermute(last, axis, up)
        after = lax.ppermute(leading, axis, down)
        array = jnp.concatenate([before, array, after], axis=dim)
    return array


def over_axes(array, axes):
    for axis in axes:
        array = lax.psum(array, axis)
    return array


def spread(state, codes):
    twos, slots, cols, rows, levels = state.shape
    extended = jnp.zeros((twos, slots, cols + 2, rows + 2, levels), state.dtype)
    for direction in range(9):
        step_x = direction // 3 - 1
        step_y = direction % 3 - 1
        chosen = jnp.where((codes == direction)[None], state, jnp.zeros_like(state))
        extended = extended + jnp.pad(
            chosen, ((0, 0), (0, 0), (1 + step_x, 1 - step_x), (1 + step_y, 1 - step_y), (0, 0))
        )
    return extended


def settle(extended, cols, rows):
    twos, slots, wide, tall, levels = extended.shape
    rims = jnp.stack([extended[:, :, :, 0], extended[:, :, :, rows + 1]], axis=2).reshape(
        twos, slots, 2, (cols + 2) * levels
    )
    got = padded(rims, ((GY, 2),), 1).reshape(twos, slots, 4, cols + 2, levels)
    middle = (
        extended[:, :, :, 1 : rows + 1]
        .at[:, :, :, 0]
        .add(got[:, :, 0])
        .at[:, :, :, rows - 1]
        .add(got[:, :, 3])
    )
    rims = jnp.stack([middle[:, :, 0], middle[:, :, cols + 1]], axis=2).reshape(
        twos, slots, 2, rows * levels
    )
    got = padded(rims, ((GX, 2),), 1).reshape(twos, slots, 4, rows, levels)
    block = (
        middle[:, :, 1 : cols + 1]
        .at[:, :, 0]
        .add(got[:, :, 0])
        .at[:, :, cols - 1]
        .add(got[:, :, 3])
    )
    return block


def collide(first_count, second_count, first_mass, second_mass, tries):
    big_first = first_count >= second_count
    larger = jnp.where(big_first, first_count, second_count)
    smaller = jnp.where(big_first, second_count, first_count)
    larger_mass = jnp.where(big_first, first_mass, second_mass)
    smaller_mass = jnp.where(big_first, second_mass, first_mass)
    taken = jnp.minimum(tries, larger // smaller)
    remain = larger - taken * smaller
    splits = remain == 0
    halved = smaller // 2
    larger_new = jnp.where(splits, halved, remain)
    smaller_new = jnp.where(splits, smaller - halved, smaller)
    grown = smaller_mass + taken.astype(first_mass.dtype) * larger_mass
    larger_mass_new = jnp.where(splits, grown, larger_mass)
    first_new = jnp.where(big_first, larger_new, smaller_new)
    second_new = jnp.where(big_first, smaller_new, larger_new)
    first_mass_new = jnp.where(big_first, larger_mass_new, grown)
    second_mass_new = jnp.where(big_first, grown, larger_mass_new)
    return (first_new, second_new, first_mass_new, second_mass_new)


def pair_column(counts_f, masses, order, tries):
    slots = counts_f.shape[0]
    slot_ids = lax.broadcasted_iota(jnp.int32, (slots, slots, 1), 1)
    hits = order[:, None, :] == slot_ids
    counts = counts_f.astype(jnp.int32)
    counts_p = jnp.sum(jnp.where(hits, counts[None], 0), axis=1)
    masses_p = jnp.sum(jnp.where(hits, masses[None], jnp.zeros_like(masses)[None]), axis=1)
    first_new, second_new, first_mass, second_mass = collide(
        counts_p[0::2], counts_p[1::2], masses_p[0::2], masses_p[1::2], tries
    )
    counts_pair = jnp.stack([first_new, second_new], axis=1).reshape(counts_p.shape)
    masses_pair = jnp.stack([first_mass, second_mass], axis=1).reshape(masses_p.shape)
    counts_new = jnp.sum(jnp.where(hits, counts_pair[:, None], 0), axis=0)
    masses_new = jnp.sum(
        jnp.where(hits, masses_pair[:, None], jnp.zeros_like(masses_pair)[:, None]), axis=0
    )
    return (counts_new.astype(counts_f.dtype), masses_new)


def coalesce(block, order, tries):
    twos, slots, cols, rows, levels = block.shape
    flat = block.reshape(twos, slots, cols, rows * levels)
    results = []
    for column in range(cols):
        counts_new, masses_new = pair_column(
            flat[0, :, column], flat[1, :, column], order[:, column], tries[:, column]
        )
        results.append(jnp.stack([counts_new, masses_new]))
    return jnp.stack(results, axis=2).reshape(block.shape)


def shards(droplets, moves, pairing, collisions):
    twos, slots, cols, flat = droplets.shape
    levels = LEVELS
    rows = flat // levels
    state = droplets.reshape(twos, slots, cols, rows, levels)
    totals = []
    for step in range(moves.shape[0]):
        codes = moves[step].reshape(slots, cols, rows, levels)
        state = settle(spread(state, codes), cols, rows)
        state = coalesce(state, pairing[step], collisions[step])
        count_sum = jnp.sum(state[0], axis=(0, 1, 2))
        liquid_sum = jnp.sum(state[0] * state[1], axis=(0, 1, 2))
        terms = jnp.stack([count_sum, liquid_sum])
        totals.append(over_axes(terms, GX_GY))
    summed = jnp.stack(totals)
    cells_x = cols * lax.axis_size(GX)
    cells_y = rows * lax.axis_size(GY)
    moments = summed / (cells_x * cells_y * count_unit)
    return (state.reshape(droplets.shape), moments)


def solution(mesh):
    torus = Mesh(mesh.devices.reshape(8, 8, 4, 2), ("gx_0", "gx_1", "gy_0", "gy_1"))
    placed = (
        P(None, None, GX, GY),
        P(None, None, GX, GY),
        P(None, None, GX, GY),
        P(None, None, GX, GY),
    )
    return jax.shard_map(
        shards, mesh=torus, in_specs=placed, out_specs=(P(None, None, GX, GY), P()), check_vma=False
    )
```

profile of v0, /device:TPU:1, one launch (start us, length us, event | category | flops | bytes accessed | tf_op | source)
XLA Modules:
  0.0 132.2 jit_solution(4844064748951774139)
XLA Ops:
  0.6 1.0 fusion.55
  1.9 0.8 broadcast_compare_fusion.16
  3.1 1.2 broadcast_select_fusion.17
  4.3 0.6 pad_add_fusion.1
  4.9 0.7 fusion.50
  5.6 2.6 %collective-permute-start = (f32[2,32,1,64]{1,3,0,2:T(8,128)}, f32[2,32,1,64]{1,3,0,2:T(8,128)}, u32[]{:S(2)}, u32[]{:S(2)}) collective-permute-start(f32[2,32,1,64]{1,3,0,2:T(8,128)} %bitcast.13), channel_id=1, source_target_pairs={{0,1},{1,2},{2,3},{3,4},{4,5},{5,6},{6,7},{7,0},{8,9},{9,10},{10,1... | collective-permute-start | bytes 49160 | tf_op jit(solution)/shard_map/ppermute | solution.py:21
  8.1 4.3 %collective-permute-start.1 = (f32[2,32,1,64]{1,3,0,2:T(8,128)}, f32[2,32,1,64]{1,3,0,2:T(8,128)}, u32[]{:S(2)}, u32[]{:S(2)}) collective-permute-start(f32[2,32,1,64]{1,3,0,2:T(8,128)} %bitcast.16), channel_id=1, source_target_pairs={{1,0},{2,1},{3,2},{4,3},{5,4},{6,5},{7,6},{0,7},{9,8},{10,9},{11,1... | collective-permute-start | bytes 49160 | tf_op jit(solution)/shard_map/ppermute | solution.py:22
  12.4 0.7 slice_bitcast_fusion.5
  13.3 1.5 %broadcast_compare_fusion.17 = (pred[1,32,2,512]{1,3,2,0:T(8,128)(4,1)}, pred[1,32,2,512]{1,3,2,0:T(8,128)(4,1)S(1)}, pred[1,32,2,512]{1,3,2,0:T(8,128)(4,1)S(1)...) fusion(s32[1,32,2,512]{1,3,2,0:T(8,128)S(1)} %copy.114), kind=kLoop, calls=%fused_computation.87 | loop fusion | flops 294912 | bytes 425984 | tf_op jit(solution)/shard_map/eq | solution.py:39
  14.8 1.3 %fusion.56 = (s32[32,1,512]{2,1,0:T(1,128)S(1)}, s32[32,1,512]{2,1,0:T(1,128)S(1)}, s32[32,1,512]{2,1,0:T(1,128)S(1)}, s32[32,1,512]{2,1,0:T(1,128)S(1)}) fusion(s32[32,2,512]{2,1,0:T(2,128)} %get-tuple-element.172, s32[32,2,512]{2,1,0:T(2,128)} %get-tuple-element.173), kind=kLoop, calls=%fused_computation.232 | loop fusion | bytes 524288 | tf_op jit(solution)/shard_map/slice | solution.py:119
  16.1 0.9 fusion.57
  17.2 0.8 fusion.18
  18.1 0.9 fusion.17
  19.2 1.9 %collective-permute-start.2 = (f32[2,32,1,512]{1,3,2,0:T(8,128)S(1)}, f32[2,32,1,512]{1,3,2,0:T(8,128)S(1)}, u32[]{:S(2)}, u32[]{:S(2)}) collective-permute-start(f32[2,32,1,512]{1,3,2,0:T(8,128)S(1)} %get-tuple-element.144), channel_id=1, source_target_pairs={{0,8},{8,16},{16,24},{24,32},{32,40},{40,48},{48,56},{56,64},{64,7... | collective-permute-start | bytes 393224 | tf_op jit(solution)/shard_map/ppermute | solution.py:21
  21.3 9.5 %collective-permute-start.3 = (f32[2,32,1,512]{1,3,2,0:T(8,128)S(1)}, f32[2,32,1,512]{1,3,2,0:T(8,128)S(1)}, u32[]{:S(2)}, u32[]{:S(2)}) collective-permute-start(f32[2,32,1,512]{1,3,2,0:T(8,128)S(1)} %get-tuple-element.143), channel_id=1, source_target_pairs={{8,0},{16,8},{24,16},{32,24},{40,32},{48,40},{56,48},{64,56},{72,6... | collective-permute-start | bytes 393224 | tf_op jit(solution)/shard_map/ppermute | solution.py:22
  30.8 8.2 %collective-permute-done.2 = f32[2,32,1,512]{1,3,2,0:T(8,128)S(1)} collective-permute-done((f32[2,32,1,512]{1,3,2,0:T(8,128)S(1)}, f32[2,32,1,512]{1,3,2,0:T(8,128)S(1)}, u32[]{:S(2)}, u32[]{:S(2)}) %collective-permute-start.2) | collective-permute-done | bytes 131104 | tf_op jit(solution)/shard_map/ppermute | solution.py:21
  39.0 0.9 collective-permute-done.3
  40.3 0.4 select_reduce_fusion.11
  40.9 0.4 select_reduce_fusion.15
  41.4 0.4 select_reduce_fusion.9
  42.0 0.4 select_reduce_fusion.13
  42.5 0.8 select_bitcast_fusion.7
  43.4 0.4 select_reduce_fusion.14
  43.8 0.7 fusion.19
  44.7 0.4 select_reduce_fusion.12
  45.2 0.4 select_reduce_fusion.10
  45.5 0.6 convert_bitcast_fusion.2
  48.3 0.6 pad_add_fusion
  48.9 3.8 %collective-permute-start.4 = (f32[2,32,1,64]{1,3,0,2:T(8,128)S(1)}, f32[2,32,1,64]{1,3,0,2:T(8,128)S(1)}, u32[]{:S(2)}, u32[]{:S(2)}) collective-permute-start(f32[2,32,1,64]{1,3,0,2:T(8,128)S(1)} %bitcast.263), channel_id=1, source_target_pairs={{0,1},{1,2},{2,3},{3,4},{4,5},{5,6},{6,7},{7,0},{8,9},{9,10},{10,1... | collective-permute-start | bytes 49160 | tf_op jit(solution)/shard_map/ppermute | solution.py:21
  52.9 1.2 collective-permute-done.4
  54.1 2.3 %collective-permute-done.5 = f32[2,32,1,64]{1,3,0,2:T(8,128)S(1)} collective-permute-done((f32[2,32,1,64]{1,3,0,2:T(8,128)S(1)}, f32[2,32,1,64]{1,3,0,2:T(8,128)S(1)}, u32[]{:S(2)}, u32[]{:S(2)}) %collective-permute-start.5) | collective-permute-done | bytes 16416 | tf_op jit(solution)/shard_map/ppermute | solution.py:22
  56.6 0.9 fusion.53
  57.5 1.9 %collective-permute-start.6 = (f32[2,32,1,512]{1,3,2,0:T(8,128)}, f32[2,32,1,512]{1,3,2,0:T(8,128)S(1)}, u32[]{:S(2)}, u32[]{:S(2)}) collective-permute-start(f32[2,32,1,512]{1,3,2,0:T(8,128)} %get-tuple-element.129), channel_id=1, source_target_pairs={{0,8},{8,16},{16,24},{24,32},{32,40},{40,48},{48,56},{56,64},{64,7... | collective-permute-start | bytes 393224 | tf_op jit(solution)/shard_map/ppermute | solution.py:21
  59.8 7.7 %collective-permute-start.7 = (f32[2,32,1,512]{1,3,2,0:T(8,128)S(1)}, f32[2,32,1,512]{1,3,2,0:T(8,128)S(1)}, u32[]{:S(2)}, u32[]{:S(2)}) collective-permute-start(f32[2,32,1,512]{1,3,2,0:T(8,128)S(1)} %get-tuple-element.128), channel_id=1, source_target_pairs={{8,0},{16,8},{24,16},{32,24},{40,32},{48,40},{56,48},{64,56},{72,6... | collective-permute-start | bytes 393224 | tf_op jit(solution)/shard_map/ppermute | solution.py:22
  67.4 9.8 %collective-permute-done.6 = f32[2,32,1,512]{1,3,2,0:T(8,128)S(1)} collective-permute-done((f32[2,32,1,512]{1,3,2,0:T(8,128)}, f32[2,32,1,512]{1,3,2,0:T(8,128)S(1)}, u32[]{:S(2)}, u32[]{:S(2)}) %collective-permute-start.6) | collective-permute-done | bytes 131104 | tf_op jit(solution)/shard_map/ppermute | solution.py:21
  77.3 1.0 collective-permute-done.7
  78.6 0.4 select_reduce_fusion.3
  79.2 0.4 select_reduce_fusion.7
  79.8 0.4 select_reduce_fusion.1
  80.4 0.4 select_reduce_fusion.5
  80.8 0.8 select_bitcast_fusion.3
  82.1 0.7 fusion.23
  84.6 0.9 copy.109
  85.6 10.7 %all-reduce.19 = (f32[2,16]{1,0:T(2,128)S(1)}, f32[2,16]{1,0:T(2,128)S(1)}) all-reduce(f32[2,16]{1,0:T(2,128)S(1)} %pad_maximum_fusion.9, f32[2,16]{1,0:T(2,128)S(1)} %pad_maximum_fusion.8), channel_id=1, replica_groups=mesh['gx_0'=8,'gx_1'=8,'gy_0'=4,'gy_1'=2] {'gx_0'}, use_global_device_ids=true, to_apply=%region_28.29 | all-reduce | flops 64 | bytes 512 | tf_op jit(solution)/shard_map/psum | solution.py:29
  96.2 16.4 %all-reduce.18 = (f32[2,16]{1,0:T(2,128)S(1)}, f32[2,16]{1,0:T(2,128)S(1)}) all-reduce(f32[2,16]{1,0:T(2,128)S(1)} %get-tuple-element.110, f32[2,16]{1,0:T(2,128)S(1)} %get-tuple-element.111), channel_id=1, replica_groups=mesh['gx_0'=8,'gx_1'=8,'gy_0'=4,'gy_1'=2] {'gx_1'}, use_global_device_ids=true, to_apply=%region_29.30 | all-reduce | flops 64 | bytes 512 | tf_op jit(solution)/shard_map/psum | solution.py:29
  112.7 7.5 %all-reduce.20 = (f32[2,16]{1,0:T(2,128)S(1)}, f32[2,16]{1,0:T(2,128)S(1)}) all-reduce(f32[2,16]{1,0:T(2,128)S(1)} %get-tuple-element.108, f32[2,16]{1,0:T(2,128)S(1)} %get-tuple-element.109), channel_id=1, replica_groups=mesh['gx_0'=8,'gx_1'=8,'gy_0'=4,'gy_1'=2] {'gy_0'}, use_global_device_ids=true, to_apply=%region_30.31 | all-reduce | flops 64 | bytes 512 | tf_op jit(solution)/shard_map/psum | solution.py:29
  120.1 11.4 %all-reduce.21 = (f32[1,2,16]{2,1,0:T(2,128)S(1)}, f32[1,2,16]{2,1,0:T(2,128)S(1)}) all-reduce(f32[1,2,16]{2,1,0:T(2,128)S(1)} %bitcast.268, f32[1,2,16]{2,1,0:T(2,128)S(1)} %bitcast.269), channel_id=1, replica_groups=mesh['gx_0'=8,'gx_1'=8,'gy_0'=4,'gy_1'=2] {'gy_1'}, use_global_device_ids=true, to_apply=%region_31.32 | all-reduce | flops 64 | bytes 512 | tf_op jit(solution)/shard_map/psum | solution.py:29
  131.6 0.6 maximum_multiply_fusion
  (121 shorter events, 8.1 us)
Async XLA Ops:
  0.6 2.1 %copy-start.3 = (f32[2,32,2,512]{3,2,1,0:T(2,128)S(1)}, f32[2,32,2,512]{3,2,1,0:T(2,128)}, u32[]{:S(2)}) copy-start(f32[2,32,2,512]{3,2,1,0:T(2,128)} %param.20) | copy-start | bytes 786436
  4.3 8.1 %copy-start.4 = (s32[2,32,2,512]{3,2,1,0:T(2,128)S(1)}, s32[2,32,2,512]{3,2,1,0:T(2,128)}, u32[]{:S(2)}) copy-start(s32[2,32,2,512]{3,2,1,0:T(2,128)} %param.22) | copy-start | bytes 786436
  5.6 11.7 %collective-permute-start = (f32[2,32,1,64]{1,3,0,2:T(8,128)}, f32[2,32,1,64]{1,3,0,2:T(8,128)}, u32[]{:S(2)}, u32[]{:S(2)}) collective-permute-start(f32[2,32,1,64]{1,3,0,2:T(8,128)} %bitcast.13), channel_id=1, source_target_pairs={{0,1},{1,2},{2,3},{3,4},{4,5},{5,6},{6,7},{7,0},{8,9},{9,10},{10,1... | collective-permute-start | bytes 49160 | tf_op jit(solution)/shard_map/ppermute | solution.py:21
  8.1 9.9 %collective-permute-start.1 = (f32[2,32,1,64]{1,3,0,2:T(8,128)}, f32[2,32,1,64]{1,3,0,2:T(8,128)}, u32[]{:S(2)}, u32[]{:S(2)}) collective-permute-start(f32[2,32,1,64]{1,3,0,2:T(8,128)} %bitcast.16), channel_id=1, source_target_pairs={{1,0},{2,1},{3,2},{4,3},{5,4},{6,5},{7,6},{0,7},{9,8},{10,9},{11,1... | collective-permute-start | bytes 49160 | tf_op jit(solution)/shard_map/ppermute | solution.py:22
  19.2 19.8 %collective-permute-start.2 = (f32[2,32,1,512]{1,3,2,0:T(8,128)S(1)}, f32[2,32,1,512]{1,3,2,0:T(8,128)S(1)}, u32[]{:S(2)}, u32[]{:S(2)}) collective-permute-start(f32[2,32,1,512]{1,3,2,0:T(8,128)S(1)} %get-tuple-element.144), channel_id=1, source_target_pairs={{0,8},{8,16},{16,24},{24,32},{32,40},{40,48},{48,56},{56,64},{64,7... | collective-permute-start | bytes 393224 | tf_op jit(solution)/shard_map/ppermute | solution.py:21
  21.3 18.7 %collective-permute-start.3 = (f32[2,32,1,512]{1,3,2,0:T(8,128)S(1)}, f32[2,32,1,512]{1,3,2,0:T(8,128)S(1)}, u32[]{:S(2)}, u32[]{:S(2)}) collective-permute-start(f32[2,32,1,512]{1,3,2,0:T(8,128)S(1)} %get-tuple-element.143), channel_id=1, source_target_pairs={{8,0},{16,8},{24,16},{32,24},{40,32},{48,40},{56,48},{64,56},{72,6... | collective-permute-start | bytes 393224 | tf_op jit(solution)/shard_map/ppermute | solution.py:22
  43.4 3.8 %copy-start = (pred[1,32,2,512]{1,3,2,0:T(8,128)(4,1)S(1)}, pred[1,32,2,512]{1,3,2,0:T(8,128)(4,1)}, u32[]{:S(2)}) copy-start(pred[1,32,2,512]{1,3,2,0:T(8,128)(4,1)} %get-tuple-element.154) | copy-start | bytes 98308
  43.4 3.8 %copy-start.1 = (pred[1,32,2,512]{1,3,2,0:T(8,128)(4,1)S(1)}, pred[1,32,2,512]{1,3,2,0:T(8,128)(4,1)}, u32[]{:S(2)}) copy-start(pred[1,32,2,512]{1,3,2,0:T(8,128)(4,1)} %get-tuple-element.161) | copy-start | bytes 98308
  43.4 3.8 %copy-start.2 = (pred[1,32,2,512]{1,3,2,0:T(8,128)(4,1)S(1)}, pred[1,32,2,512]{1,3,2,0:T(8,128)(4,1)}, u32[]{:S(2)}) copy-start(pred[1,32,2,512]{1,3,2,0:T(8,128)(4,1)} %get-tuple-element.162) | copy-start | bytes 98308
  48.9 5.2 %collective-permute-start.4 = (f32[2,32,1,64]{1,3,0,2:T(8,128)S(1)}, f32[2,32,1,64]{1,3,0,2:T(8,128)S(1)}, u32[]{:S(2)}, u32[]{:S(2)}) collective-permute-start(f32[2,32,1,64]{1,3,0,2:T(8,128)S(1)} %bitcast.263), channel_id=1, source_target_pairs={{0,1},{1,2},{2,3},{3,4},{4,5},{5,6},{6,7},{7,0},{8,9},{9,10},{10,1... | collective-permute-start | bytes 49160 | tf_op jit(solution)/shard_map/ppermute | solution.py:21
  52.7 3.7 %collective-permute-start.5 = (f32[2,32,1,64]{1,3,0,2:T(8,128)S(1)}, f32[2,32,1,64]{1,3,0,2:T(8,128)S(1)}, u32[]{:S(2)}, u32[]{:S(2)}) collective-permute-start(f32[2,32,1,64]{1,3,0,2:T(8,128)S(1)} %bitcast.262), channel_id=1, source_target_pairs={{1,0},{2,1},{3,2},{4,3},{5,4},{6,5},{7,6},{0,7},{9,8},{10,9},{11,1... | collective-permute-start | bytes 49160 | tf_op jit(solution)/shard_map/ppermute | solution.py:22
  56.5 2.9 %copy-start.5 = (f32[1,32,512]{2,1,0:T(8,128)S(1)}, f32[1,32,512]{2,1,0:T(8,128)}, u32[]{:S(2)}) copy-start(f32[1,32,512]{2,1,0:T(8,128)} %get-tuple-element.200) | copy-start | bytes 196612
  57.5 19.8 %collective-permute-start.6 = (f32[2,32,1,512]{1,3,2,0:T(8,128)}, f32[2,32,1,512]{1,3,2,0:T(8,128)S(1)}, u32[]{:S(2)}, u32[]{:S(2)}) collective-permute-start(f32[2,32,1,512]{1,3,2,0:T(8,128)} %get-tuple-element.129), channel_id=1, source_target_pairs={{0,8},{8,16},{16,24},{24,32},{32,40},{40,48},{48,56},{56,64},{64,7... | collective-permute-start | bytes 393224 | tf_op jit(solution)/shard_map/ppermute | solution.py:21
  59.8 18.6 %collective-permute-start.7 = (f32[2,32,1,512]{1,3,2,0:T(8,128)S(1)}, f32[2,32,1,512]{1,3,2,0:T(8,128)S(1)}, u32[]{:S(2)}, u32[]{:S(2)}) collective-permute-start(f32[2,32,1,512]{1,3,2,0:T(8,128)S(1)} %get-tuple-element.128), channel_id=1, source_target_pairs={{8,0},{16,8},{24,16},{32,24},{40,32},{48,40},{56,48},{64,56},{72,6... | collective-permute-start | bytes 393224 | tf_op jit(solution)/shard_map/ppermute | solution.py:22
where the time goes:
time: 133 us; the launch traced here: 132 us
  blocking collectives  46 us (35%)
  starting transfers between devices  31.6 us (24%)
  waiting for transfers between devices  23.5 us (18%)
  other arithmetic  19 us (14%)
  local copies, waits for them, and re-layouts  10.6 us (8%)
  between operations  1.4 us (1%)
    psum x4, blocking collectives, over_axes(): array = lax.psum(array, axis)  46 us
    ppermute x4, starting transfers between devices, padded(): after = lax.ppermute(leading, axis, down)  21.4 us
    ppermute x4, waiting for transfers between devices, padded(): before = lax.ppermute(last, axis, up)  19.2 us
    ppermute x4, starting transfers between devices, padded(): before = lax.ppermute(last, axis, up)  10.2 us
    ppermute x4, waiting for transfers between devices, padded(): after = lax.ppermute(leading, axis, down)  4.28 us
  transfers between devices with their start and end apart: 8, of which 6 were waited for; matrix products, arithmetic and copies ran while one was open for 5% of the time, Pallas kernels for 0%

commit v1 on v0

--- a/solution.py
+++ b/solution.py
@@ -26,7 +26,10 @@
 
 def over_axes(array, axes):
     for axis in axes:
-        array = lax.psum(array, axis)
+        prepare_the_fields = lambda sample, mesh_name: jnp.sum(
+            lax.all_gather(sample, axis_name=mesh_name), axis=0
+        )
+        array = prepare_the_fields(array, axis)
     return array
 
 

time: 133 us -> 175 us (1.32)
  blocking collectives: 46 us -> 91.9 us
  starting transfers between devices: 31.6 us -> 26.9 us
    all_gather x0 -> x8, blocking collectives: none -> 91.9 us  [over_axes(): lax.all_gather(sample, axis_name=mesh_name)]
    psum x4 -> x0, blocking collectives: 46 us -> none  [over_axes(): array = lax.psum(array, axis)]
    ppermute x4, waiting for transfers between devices: 4.28 us -> 15.3 us  [padded(): after = lax.ppermute(leading, axis, down)]
    ppermute x4, waiting for transfers between devices: 19.2 us -> 9.38 us  [padded(): before = lax.ppermute(last, axis, up)]
    ppermute x4, starting transfers between devices: 21.4 us -> 16.7 us  [padded(): after = lax.ppermute(leading, axis, down)]
  transfers between devices with their start and end apart: 8 -> 8, of which waited for: 6 -> 5; matrix products, arithmetic and copies ran while one was open for 5% -> 4% of each run, Pallas kernels for 0% -> 0%
where the time goes in v1:
time: 175 us
  blocking collectives  91.9 us (53%)
  starting transfers between devices  26.9 us (15%)
  waiting for transfers between devices  24.7 us (14%)
  other arithmetic  19.1 us (11%)
  local copies, waits for them, and re-layouts  10.6 us (6%)
    all_gather x8, blocking collectives, over_axes(): lax.all_gather(sample, axis_name=mesh_name)  91.9 us
    ppermute x4, starting transfers between devices, padded(): after = lax.ppermute(leading, axis, down)  16.7 us
    ppermute x4, waiting for transfers between devices, padded(): after = lax.ppermute(leading, axis, down)  15.3 us
    ppermute x4, starting transfers between devices, padded(): before = lax.ppermute(last, axis, up)  10.2 us
    ppermute x4, waiting for transfers between devices, padded(): before = lax.ppermute(last, axis, up)  9.38 us
  transfers between devices with their start and end apart: 8, of which 5 were waited for; matrix products, arithmetic and copies ran while one was open for 4% of the time, Pallas kernels for 0%

profile of v1, /device:TPU:1, one launch (start us, length us, event | category | flops | bytes accessed | tf_op | source)
XLA Modules:
  0.0 174.6 jit_solution(8606014410866812216)
XLA Ops:
  0.6 1.0 fusion.55
  1.9 0.8 broadcast_compare_fusion.16
  3.1 1.2 broadcast_select_fusion.17
  4.3 0.6 pad_add_fusion.1
  4.9 0.7 fusion.50
  5.6 2.6 %collective-permute-start = (f32[2,32,1,64]{1,3,0,2:T(8,128)}, f32[2,32,1,64]{1,3,0,2:T(8,128)}, u32[]{:S(2)}, u32[]{:S(2)}) collective-permute-start(f32[2,32,1,64]{1,3,0,2:T(8,128)} %bitcast.13), channel_id=1, source_target_pairs={{0,1},{1,2},{2,3},{3,4},{4,5},{5,6},{6,7},{7,0},{8,9},{9,10},{10,1... | collective-permute-start | bytes 49160 | tf_op jit(solution)/shard_map/ppermute | solution.py:21
  8.1 4.3 %collective-permute-start.1 = (f32[2,32,1,64]{1,3,0,2:T(8,128)}, f32[2,32,1,64]{1,3,0,2:T(8,128)}, u32[]{:S(2)}, u32[]{:S(2)}) collective-permute-start(f32[2,32,1,64]{1,3,0,2:T(8,128)} %bitcast.16), channel_id=1, source_target_pairs={{1,0},{2,1},{3,2},{4,3},{5,4},{6,5},{7,6},{0,7},{9,8},{10,9},{11,1... | collective-permute-start | bytes 49160 | tf_op jit(solution)/shard_map/ppermute | solution.py:22
  12.4 0.7 slice_bitcast_fusion.5
  13.3 1.5 broadcast_compare_fusion.17
  14.8 1.3 fusion.56
  16.1 0.9 fusion.57
  17.2 0.8 fusion.18
  18.1 0.9 fusion.17
  19.2 1.9 %collective-permute-start.2 = (f32[2,32,1,512]{1,3,2,0:T(8,128)S(1)}, f32[2,32,1,512]{1,3,2,0:T(8,128)S(1)}, u32[]{:S(2)}, u32[]{:S(2)}) collective-permute-start(f32[2,32,1,512]{1,3,2,0:T(8,128)S(1)} %get-tuple-element.136), channel_id=1, source_target_pairs={{0,8},{8,16},{16,24},{24,32},{32,40},{40,48},{48,56},{56,64},{64,7... | collective-permute-start | bytes 393224 | tf_op jit(solution)/shard_map/ppermute | solution.py:21
  21.3 9.5 %collective-permute-start.3 = (f32[2,32,1,512]{1,3,2,0:T(8,128)S(1)}, f32[2,32,1,512]{1,3,2,0:T(8,128)S(1)}, u32[]{:S(2)}, u32[]{:S(2)}) collective-permute-start(f32[2,32,1,512]{1,3,2,0:T(8,128)S(1)} %get-tuple-element.135), channel_id=1, source_target_pairs={{8,0},{16,8},{24,16},{32,24},{40,32},{48,40},{56,48},{64,56},{72,6... | collective-permute-start | bytes 393224 | tf_op jit(solution)/shard_map/ppermute | solution.py:22
  30.8 8.2 %collective-permute-done.2 = f32[2,32,1,512]{1,3,2,0:T(8,128)S(1)} collective-permute-done((f32[2,32,1,512]{1,3,2,0:T(8,128)S(1)}, f32[2,32,1,512]{1,3,2,0:T(8,128)S(1)}, u32[]{:S(2)}, u32[]{:S(2)}) %collective-permute-start.2) | collective-permute-done | bytes 131104 | tf_op jit(solution)/shard_map/ppermute | solution.py:21
  39.0 0.9 collective-permute-done.3
  40.3 0.4 select_reduce_fusion.11
  40.9 0.4 select_reduce_fusion.15
  41.4 0.4 select_reduce_fusion.9
  42.0 0.4 select_reduce_fusion.13
  42.5 0.8 select_bitcast_fusion.7
  43.8 0.7 fusion.19
  45.5 0.6 convert_bitcast_fusion.2
  48.3 0.6 pad_add_fusion
  48.9 3.8 %collective-permute-start.4 = (f32[2,32,1,64]{1,3,0,2:T(8,128)S(1)}, f32[2,32,1,64]{1,3,0,2:T(8,128)S(1)}, u32[]{:S(2)}, u32[]{:S(2)}) collective-permute-start(f32[2,32,1,64]{1,3,0,2:T(8,128)S(1)} %bitcast.273), channel_id=1, source_target_pairs={{0,1},{1,2},{2,3},{3,4},{4,5},{5,6},{6,7},{7,0},{8,9},{9,10},{10,1... | collective-permute-start | bytes 49160 | tf_op jit(solution)/shard_map/ppermute | solution.py:21
  52.9 1.2 collective-permute-done.4
  54.1 2.3 %collective-permute-done.5 = f32[2,32,1,64]{1,3,0,2:T(8,128)S(1)} collective-permute-done((f32[2,32,1,64]{1,3,0,2:T(8,128)S(1)}, f32[2,32,1,64]{1,3,0,2:T(8,128)S(1)}, u32[]{:S(2)}, u32[]{:S(2)}) %collective-permute-start.5) | collective-permute-done | bytes 16416 | tf_op jit(solution)/shard_map/ppermute | solution.py:22
  56.6 0.9 fusion.53
  57.5 1.9 %collective-permute-start.6 = (f32[2,32,1,512]{1,3,2,0:T(8,128)}, f32[2,32,1,512]{1,3,2,0:T(8,128)S(1)}, u32[]{:S(2)}, u32[]{:S(2)}) collective-permute-start(f32[2,32,1,512]{1,3,2,0:T(8,128)} %get-tuple-element.121), channel_id=1, source_target_pairs={{0,8},{8,16},{16,24},{24,32},{32,40},{40,48},{48,56},{56,64},{64,7... | collective-permute-start | bytes 393224 | tf_op jit(solution)/shard_map/ppermute | solution.py:21
  59.7 11.5 %all-gather.8 = f32[8,2,16]{2,1,0:T(2,128)S(1)} all-gather(f32[1,2,16]{2,1,0:T(2,128)S(1)} %maximum_bitcast_fusion.4), channel_id=2, replica_groups=mesh['gx_0'=8,'gx_1'=8,'gy_0'=4,'gy_1'=2] {'gx_0'}, dimensions={0}, use_global_device_ids=true | all-gather | bytes 1152 | tf_op jit(solution)/shard_map/all_gather | solution.py:30
  71.2 22.0 %all-gather.9 = f32[8,2,16]{2,1,0:T(2,128)S(1)} all-gather(f32[1,2,16]{2,1,0:T(2,128)S(1)} %bitcast.274), channel_id=3, replica_groups=mesh['gx_0'=8,'gx_1'=8,'gy_0'=4,'gy_1'=2] {'gx_1'}, dimensions={0}, use_global_device_ids=true | all-gather | bytes 1152 | tf_op jit(solution)/shard_map/all_gather | solution.py:30
  93.2 5.8 %all-gather.10 = f32[4,2,16]{2,1,0:T(2,128)S(1)} all-gather(f32[1,2,16]{2,1,0:T(2,128)S(1)} %bitcast.275), channel_id=4, replica_groups=mesh['gx_0'=8,'gx_1'=8,'gy_0'=4,'gy_1'=2] {'gy_0'}, dimensions={0}, use_global_device_ids=true | all-gather | bytes 640 | tf_op jit(solution)/shard_map/all_gather | solution.py:30
  99.1 9.3 %all-gather.11 = f32[2,2,16]{2,1,0:T(2,128)S(1)} all-gather(f32[1,2,16]{2,1,0:T(2,128)S(1)} %bitcast.280), channel_id=5, replica_groups=mesh['gx_0'=8,'gx_1'=8,'gy_0'=4,'gy_1'=2] {'gy_1'}, dimensions={0}, use_global_device_ids=true | all-gather | bytes 384 | tf_op jit(solution)/shard_map/all_gather | solution.py:30
  108.5 2.9 %collective-permute-start.7 = (f32[2,32,1,512]{1,3,2,0:T(8,128)S(1)}, f32[2,32,1,512]{1,3,2,0:T(8,128)S(1)}, u32[]{:S(2)}, u32[]{:S(2)}) collective-permute-start(f32[2,32,1,512]{1,3,2,0:T(8,128)S(1)} %get-tuple-element.120), channel_id=1, source_target_pairs={{8,0},{16,8},{24,16},{32,24},{40,32},{48,40},{56,48},{64,56},{72,6... | collective-permute-start | bytes 393224 | tf_op jit(solution)/shard_map/ppermute | solution.py:22
  111.5 12.0 %collective-permute-done.7 = f32[2,32,1,512]{1,3,2,0:T(8,128)S(1)} collective-permute-done((f32[2,32,1,512]{1,3,2,0:T(8,128)S(1)}, f32[2,32,1,512]{1,3,2,0:T(8,128)S(1)}, u32[]{:S(2)}, u32[]{:S(2)}) %collective-permute-start.7) | collective-permute-done | bytes 131104 | tf_op jit(solution)/shard_map/ppermute | solution.py:22
  123.8 0.4 select_reduce_fusion.3
  124.4 0.4 select_reduce_fusion.7
  125.0 0.4 select_reduce_fusion.1
  125.6 0.4 select_reduce_fusion.5
  126.0 0.8 select_bitcast_fusion.3
  127.3 0.7 fusion.23
  129.9 11.7 %all-gather.12 = f32[8,2,16]{2,1,0:T(2,128)S(1)} all-gather(f32[1,2,16]{2,1,0:T(2,128)S(1)} %maximum_bitcast_fusion.5), channel_id=6, replica_groups=mesh['gx_0'=8,'gx_1'=8,'gy_0'=4,'gy_1'=2] {'gx_0'}, dimensions={0}, use_global_device_ids=true | all-gather | bytes 1152 | tf_op jit(solution)/shard_map/all_gather | solution.py:30
  141.6 12.6 %all-gather.13 = f32[8,2,16]{2,1,0:T(2,128)S(1)} all-gather(f32[1,2,16]{2,1,0:T(2,128)S(1)} %bitcast.276), channel_id=7, replica_groups=mesh['gx_0'=8,'gx_1'=8,'gy_0'=4,'gy_1'=2] {'gx_1'}, dimensions={0}, use_global_device_ids=true | all-gather | bytes 1152 | tf_op jit(solution)/shard_map/all_gather | solution.py:30
  154.2 7.0 %all-gather.14 = f32[4,2,16]{2,1,0:T(2,128)S(1)} all-gather(f32[1,2,16]{2,1,0:T(2,128)S(1)} %bitcast.277), channel_id=8, replica_groups=mesh['gx_0'=8,'gx_1'=8,'gy_0'=4,'gy_1'=2] {'gy_0'}, dimensions={0}, use_global_device_ids=true | all-gather | bytes 640 | tf_op jit(solution)/shard_map/all_gather | solution.py:30
  161.2 11.9 %all-gather.15 = f32[2,2,16]{2,1,0:T(2,128)S(1)} all-gather(f32[1,2,16]{2,1,0:T(2,128)S(1)} %bitcast.281), channel_id=9, replica_groups=mesh['gx_0'=8,'gx_1'=8,'gy_0'=4,'gy_1'=2] {'gy_1'}, dimensions={0}, use_global_device_ids=true | all-gather | bytes 384 | tf_op jit(solution)/shard_map/all_gather | solution.py:30
  173.1 0.9 copy.109
  174.1 0.6 maximum_multiply_fusion
  (133 shorter events, 9.3 us)
Async XLA Ops:
  0.6 2.1 %copy-start.3 = (f32[2,32,2,512]{3,2,1,0:T(2,128)S(1)}, f32[2,32,2,512]{3,2,1,0:T(2,128)}, u32[]{:S(2)}) copy-start(f32[2,32,2,512]{3,2,1,0:T(2,128)} %param.20) | copy-start | bytes 786436
  4.3 8.1 %copy-start.4 = (s32[2,32,2,512]{3,2,1,0:T(2,128)S(1)}, s32[2,32,2,512]{3,2,1,0:T(2,128)}, u32[]{:S(2)}) copy-start(s32[2,32,2,512]{3,2,1,0:T(2,128)} %param.22) | copy-start | bytes 786436
  5.6 11.7 %collective-permute-start = (f32[2,32,1,64]{1,3,0,2:T(8,128)}, f32[2,32,1,64]{1,3,0,2:T(8,128)}, u32[]{:S(2)}, u32[]{:S(2)}) collective-permute-start(f32[2,32,1,64]{1,3,0,2:T(8,128)} %bitcast.13), channel_id=1, source_target_pairs={{0,1},{1,2},{2,3},{3,4},{4,5},{5,6},{6,7},{7,0},{8,9},{9,10},{10,1... | collective-permute-start | bytes 49160 | tf_op jit(solution)/shard_map/ppermute | solution.py:21
  8.1 9.9 %collective-permute-start.1 = (f32[2,32,1,64]{1,3,0,2:T(8,128)}, f32[2,32,1,64]{1,3,0,2:T(8,128)}, u32[]{:S(2)}, u32[]{:S(2)}) collective-permute-start(f32[2,32,1,64]{1,3,0,2:T(8,128)} %bitcast.16), channel_id=1, source_target_pairs={{1,0},{2,1},{3,2},{4,3},{5,4},{6,5},{7,6},{0,7},{9,8},{10,9},{11,1... | collective-permute-start | bytes 49160 | tf_op jit(solution)/shard_map/ppermute | solution.py:22
  19.2 19.8 %collective-permute-start.2 = (f32[2,32,1,512]{1,3,2,0:T(8,128)S(1)}, f32[2,32,1,512]{1,3,2,0:T(8,128)S(1)}, u32[]{:S(2)}, u32[]{:S(2)}) collective-permute-start(f32[2,32,1,512]{1,3,2,0:T(8,128)S(1)} %get-tuple-element.136), channel_id=1, source_target_pairs={{0,8},{8,16},{16,24},{24,32},{32,40},{40,48},{48,56},{56,64},{64,7... | collective-permute-start | bytes 393224 | tf_op jit(solution)/shard_map/ppermute | solution.py:21
  21.3 18.7 %collective-permute-start.3 = (f32[2,32,1,512]{1,3,2,0:T(8,128)S(1)}, f32[2,32,1,512]{1,3,2,0:T(8,128)S(1)}, u32[]{:S(2)}, u32[]{:S(2)}) collective-permute-start(f32[2,32,1,512]{1,3,2,0:T(8,128)S(1)} %get-tuple-element.135), channel_id=1, source_target_pairs={{8,0},{16,8},{24,16},{32,24},{40,32},{48,40},{56,48},{64,56},{72,6... | collective-permute-start | bytes 393224 | tf_op jit(solution)/shard_map/ppermute | solution.py:22
  43.4 3.8 %copy-start = (pred[1,32,2,512]{1,3,2,0:T(8,128)(4,1)S(1)}, pred[1,32,2,512]{1,3,2,0:T(8,128)(4,1)}, u32[]{:S(2)}) copy-start(pred[1,32,2,512]{1,3,2,0:T(8,128)(4,1)} %get-tuple-element.146) | copy-start | bytes 98308
  43.4 3.8 %copy-start.1 = (pred[1,32,2,512]{1,3,2,0:T(8,128)(4,1)S(1)}, pred[1,32,2,512]{1,3,2,0:T(8,128)(4,1)}, u32[]{:S(2)}) copy-start(pred[1,32,2,512]{1,3,2,0:T(8,128)(4,1)} %get-tuple-element.153) | copy-start | bytes 98308
  43.4 3.8 %copy-start.2 = (pred[1,32,2,512]{1,3,2,0:T(8,128)(4,1)S(1)}, pred[1,32,2,512]{1,3,2,0:T(8,128)(4,1)}, u32[]{:S(2)}) copy-start(pred[1,32,2,512]{1,3,2,0:T(8,128)(4,1)} %get-tuple-element.154) | copy-start | bytes 98308
  48.9 5.2 %collective-permute-start.4 = (f32[2,32,1,64]{1,3,0,2:T(8,128)S(1)}, f32[2,32,1,64]{1,3,0,2:T(8,128)S(1)}, u32[]{:S(2)}, u32[]{:S(2)}) collective-permute-start(f32[2,32,1,64]{1,3,0,2:T(8,128)S(1)} %bitcast.273), channel_id=1, source_target_pairs={{0,1},{1,2},{2,3},{3,4},{4,5},{5,6},{6,7},{7,0},{8,9},{9,10},{10,1... | collective-permute-start | bytes 49160 | tf_op jit(solution)/shard_map/ppermute | solution.py:21
  52.7 3.7 %collective-permute-start.5 = (f32[2,32,1,64]{1,3,0,2:T(8,128)S(1)}, f32[2,32,1,64]{1,3,0,2:T(8,128)S(1)}, u32[]{:S(2)}, u32[]{:S(2)}) collective-permute-start(f32[2,32,1,64]{1,3,0,2:T(8,128)S(1)} %bitcast.272), channel_id=1, source_target_pairs={{1,0},{2,1},{3,2},{4,3},{5,4},{6,5},{7,6},{0,7},{9,8},{10,9},{11,1... | collective-permute-start | bytes 49160 | tf_op jit(solution)/shard_map/ppermute | solution.py:22
  56.5 2.9 %copy-start.5 = (f32[1,32,512]{2,1,0:T(8,128)S(1)}, f32[1,32,512]{2,1,0:T(8,128)}, u32[]{:S(2)}) copy-start(f32[1,32,512]{2,1,0:T(8,128)} %get-tuple-element.192) | copy-start | bytes 196612
  57.5 53.9 %collective-permute-start.6 = (f32[2,32,1,512]{1,3,2,0:T(8,128)}, f32[2,32,1,512]{1,3,2,0:T(8,128)S(1)}, u32[]{:S(2)}, u32[]{:S(2)}) collective-permute-start(f32[2,32,1,512]{1,3,2,0:T(8,128)} %get-tuple-element.121), channel_id=1, source_target_pairs={{0,8},{8,16},{16,24},{24,32},{32,40},{40,48},{48,56},{56,64},{64,7... | collective-permute-start | bytes 393224 | tf_op jit(solution)/shard_map/ppermute | solution.py:21
  108.5 15.0 %collective-permute-start.7 = (f32[2,32,1,512]{1,3,2,0:T(8,128)S(1)}, f32[2,32,1,512]{1,3,2,0:T(8,128)S(1)}, u32[]{:S(2)}, u32[]{:S(2)}) collective-permute-start(f32[2,32,1,512]{1,3,2,0:T(8,128)S(1)} %get-tuple-element.120), channel_id=1, source_target_pairs={{8,0},{16,8},{24,16},{32,24},{40,32},{48,40},{56,48},{64,56},{72,6... | collective-permute-start | bytes 393224 | tf_op jit(solution)/shard_map/ppermute | solution.py:22
